TPU v7x, 32 devices: a whole 2x2x4 slice. The times are simulated.
32 devices in a mesh: groups: 2 (over y), gx: 4 (over z), gy: 4 (over x, core).
Axes of the slice: x: 2, y: 2, z: 4, core: 2. Of those that a mesh axis runs over, the one named last changes fastest.
Arguments:
- tokens: bfloat16 [2, 16, 16384], P(None, 'groups', 'gx'), parts along dimension 1, may hold values from -20 to 20, as said below
- lengths: int32 [2, 16], P(None, ('groups', 'gx')), parts along dimension 1, may hold values from 1 to 1024, as said below
- norm_gain: bfloat16 [16384], P('gx'), may hold values from 0.5 to 2
- w_query: bfloat16 [16384, 8192], P('gx', 'gy'), may hold values from -1.171875 to 1.171875
- key_value_weight: bfloat16 [16384, 4, 256], P('gx', 'gy'), may hold values from -0.046875 to 0.046875
- w_out: bfloat16 [8192, 16384], P('gy', 'gx'), may hold values from -0.0625 to 0.0625
- cache: bfloat16 [2, 16, 1024, 4, 2, 128], P(None, ('groups', 'gx'), None, 'gy'), parts along dimension 1, may hold values from -16 to 16
Outputs:
- layer_out: bfloat16 [2, 16, 16384], P(None, 'groups', 'gx'), parts along dimension 1
There are 2 independent parts, one for each index of `groups`. A program takes and returns all parts, laid end to end along the dimension named above; an argument that names none is the same for every part. Nothing has to cross between parts.
Inputs may be any that keep to these rules, and one draw needn't show every extreme that they name: `tokens`: entries vary with the feature and the row. `lengths`: some rollout has exactly 1024 cached positions in every draw.
All inputs are finite; a program needn't handle non-finite values.
Results may differ from a plain program's by a relative error of at most 0.012.
The roundings to bfloat16 on the way count: a program that leaves them out, or rounds other values in their place, can miss the bound.
Values may be sent and summed in bfloat16 or wider, within the bound.
No kernel may reach another device: no remote copies, remote signals or barrier semaphores. Data moves between devices by JAX's collectives and lax.ppermute only.
A program may use at most 128 MiB of HBM per device.

v0:
```python
import jax
import jax.numpy as jnp
from jax import lax
from jax.sharding import PartitionSpec as P

MODEL_WIDTH = 16384
HEAD_SIZE = 128


def rotate(vectors, positions):
    half = vectors.shape[-1] // 2
    freq = 500000.0 ** (-2.0 * jnp.arange(half, dtype=jnp.float32) / vectors.shape[-1])
    angle = positions[..., None] * freq
    cosine = jnp.cos(angle)
    sine = jnp.sin(angle)
    first = vectors[..., :half]
    second = vectors[..., half:]
    return jnp.concatenate(
        [first * cosine - second * sine, second * cosine + first * sine], axis=-1
    )


def attend(query_sum, keyval_sum, local_squares, lengths, cache):
    batches, rows_here = lengths.shape
    score_scale = lax.rsqrt(local_squares / MODEL_WIDTH + 1e-05)
    heads_kv = keyval_sum.shape[2]
    query_group = query_sum.shape[2] // (heads_kv * HEAD_SIZE)
    query = (
        query_sum.reshape(batches, rows_here, heads_kv, query_group, HEAD_SIZE)
        * score_scale[:, :, None, None, None]
    )
    key_value = keyval_sum * score_scale[:, :, None, None]
    positions = lengths.astype(jnp.float32)
    rotated_query = rotate(query, positions[:, :, None, None]).astype(jnp.bfloat16)
    rkey = rotate(key_value[..., :HEAD_SIZE], positions[:, :, None])
    value_new = key_value[..., HEAD_SIZE:]
    inv_root = 1.0 / jnp.sqrt(jnp.float32(HEAD_SIZE))
    keys = cache[:, :, :, :, 0, :]
    values = cache[:, :, :, :, 1, :]
    scores = (
        jnp.einsum("mrkgd,mrskd->mrkgs", rotated_query, keys, preferred_element_type=jnp.float32)
        * inv_root
    )
    valid = jnp.arange(cache.shape[2], dtype=jnp.int32)[None, None, :] < lengths[:, :, None]
    scores = jnp.where(valid[:, :, None, None, :], scores, -1e30)
    new_score = (
        jnp.sum(rotated_query.astype(jnp.float32) * rkey[:, :, :, None, :], axis=-1) * inv_root
    )
    top = jnp.maximum(jnp.max(scores, axis=-1), new_score)
    weights = jnp.exp(scores - top[..., None])
    new_weight = jnp.exp(new_score - top)
    total = jnp.sum(weights, axis=-1) + new_weight
    summed = jnp.einsum(
        "mrkgs,mrskd->mrkgd",
        weights.astype(jnp.bfloat16),
        values,
        preferred_element_type=jnp.float32,
    )
    summed = summed + new_weight[..., None] * value_new[:, :, :, None, :]
    return (
        (summed / total[..., None])
        .astype(jnp.bfloat16)
        .reshape(batches, rows_here, heads_kv * query_group * HEAD_SIZE)
    )


def local(tokens, lengths, norm_gain, w_query, key_value_weight, w_out, cache):
    x_full = tokens.astype(jnp.float32)
    squares = jnp.sum(x_full * x_full, axis=-1)
    normed = (x_full * norm_gain.astype(jnp.float32)).astype(jnp.bfloat16)
    query_part = jnp.einsum("mrd,dc->mrc", normed, w_query, preferred_element_type=jnp.float32)
    keyval_part = jnp.einsum(
        "mrd,dkc->mrkc", normed, key_value_weight, preferred_element_type=jnp.float32
    )
    query_sum, keyval_sum, local_squares = (
        lax.psum_scatter(query_part, "gx", scatter_dimension=1, tiled=True),
        lax.psum_scatter(keyval_part, "gx", scatter_dimension=1, tiled=True),
        lax.psum_scatter(squares, "gx", scatter_dimension=1, tiled=True),
    )
    attended = attend(query_sum, keyval_sum, local_squares, lengths, cache)
    projected = jnp.einsum(
        "mrc,cd->mrd",
        lax.all_gather(attended, "gx", axis=1, tiled=True),
        w_out,
        preferred_element_type=jnp.float32,
    )
    summed_heads = lax.psum(projected, "gy")
    return (x_full + summed_heads).astype(jnp.bfloat16)


def solution(mesh):
    placed = (
        P(None, "groups", "gx"),
        P(None, ("groups", "gx")),
        P("gx"),
        P("gx", "gy"),
        P("gx", "gy", None),
        P("gy", "gx"),
        P(None, ("groups", "gx"), None, "gy", None, None),
    )
    return jax.shard_map(
        local, mesh=mesh, in_specs=placed, out_specs=P(None, "groups", "gx"), check_vma=False
    )
```

profile of v0, /device:TPU:0, one launch (start us, length us, event | category | flops | bytes accessed | tf_op | source)
XLA Modules:
  0.0 122.0 jit_solution(11372717634072038642)
XLA Ops:
  6.5 0.0 copy-start
  6.5 0.0 all-reduce.9.cloned.1.call-start
  6.5 0.8 convert_element_type.46
  7.4 0.0 copy-start.1
  7.4 0.0 copy-start.2
  7.4 8.8 %fusion.2 = f32[2,8,2048]{2,1,0:T(8,128)} fusion(bf16[4096,2048]{1,0:T(8,128)(2,1)} %param.10, bf16[2,8,4096]{2,1,0:T(8,128)(2,1)} %param.7, f32[4096]{0:T(1024)S(1)} %convert_element_type.46), kind=kOutput, calls=%fused_computation.2 | convolution fusion | flops 268632064 | bytes 17055744 | tf_op jit(solution)/shard_map/mrd,dc->mrc/dot_general | solution.py:71
  16.2 0.0 copy-start.3
  16.2 0.0 all-reduce.9.cloned.1.call-update
  16.2 0.0 all-reduce.7.cloned.1.call-start
  16.3 0.0 copy-done.1
  16.3 0.1 fusion.13
  16.4 0.0 copy-done.2
  16.4 0.1 iota_compare_fusion
  16.5 0.0 copy-done
  16.5 0.4 fusion.9
  16.9 0.0 copy-done.3
  16.9 0.7 dynamic-slice
  18.3 0.1 multiply_cosine_fusion.1
  18.4 20.8 %all-reduce.3 = (f32[2,8]{1,0:T(2,128)S(1)}, f32[2,8,1,256]{3,1,0,2:T(8,128)S(1)}) all-reduce(f32[2,8]{1,0:T(2,128)S(1)} %fusion.13, f32[2,8,1,256]{3,1,0,2:T(8,128)S(1)} %fusion.9), channel_id=3, replica_groups=mesh['groups'=2,'gx'=4,'gy'=4] {'gx'}, use_global_device_ids=true, to_apply=%region_2.0.clone | all-reduce | flops 4112 | bytes 32896
  39.2 0.1 fusion.32
  39.3 0.1 dynamic-slice_multiply_fusion
  39.4 0.1 fusion.29
  39.5 6.9 %fusion.35 = (bf16[2,2,1024,1,1,128]{5,4,3,2,1,0:T(2,128)(2,1)}, bf16[2,2,1024,1,1,128]{5,4,3,2,1,0:T(2,128)(2,1)}) fusion(bf16[2,2,1024,1,2,128]{5,4,3,2,1,0:T(2,128)(2,1)} %param.13), kind=kLoop, calls=%fused_computation.55 | loop fusion | bytes 4194304 | tf_op jit(solution)/shard_map/slice | solution.py:38
  46.4 0.1 maximum_bitcast_fusion
  46.5 7.3 %all-reduce.9.cloned.1.call-done = f32[2,8,2048]{2,1,0:T(8,128)} async-done(((f32[2,8,2048]{2,1,0:T(8,128)}), f32[2,8,2048]{2,1,0:T(8,128)}) %all-reduce.9.cloned.1.call-update) | async-done | bytes 131088
  53.9 0.9 constant_dynamic-slice_fusion
  54.8 0.1 broadcast_multiply_fusion
  54.9 0.1 subtract_convert_fusion
  55.0 0.2 multiply_reduce_fusion
  55.1 2.1 %fusion.36 = (f32[2,2,16]{2,1,0:T(2,128)S(1)}, f32[2,2,16,1024]{3,2,1,0:T(8,128)S(1)}) fusion(bf16[2,2,1024,1,1,128]{5,4,3,2,1,0:T(2,128)(2,1)} %get-tuple-element.9, bf16[2,2,16,64]{3,2,1,0:T(8,128)(2,1)S(1)} %bitcast.38, bf16[2,2,16,64]{3,2,1,0:T(8,128)(2,1)S(1)} %bitcast.37, pred[2,2,1024]{2,1,0:T(4,128)(4,1)S(1)} %iota_compare_fusion), kind=kOutput, calls=%fused_computation.56 | convolution fusion | flops 17006528 | bytes 1331456 | tf_op jit(solution)/shard_map/mrkgd,mrskd->mrkgs/dot_general | solution.py:41
  57.3 0.2 fusion.15
  57.5 1.9 %fusion.8 = bf16[2,2,16,128]{3,2,1,0:T(8,128)(2,1)S(1)} fusion(bf16[2,2,1024,1,1,128]{5,4,3,2,1,0:T(2,128)(2,1)} %get-tuple-element.10, f32[2,2,16,1024]{3,2,1,0:T(8,128)S(1)} %get-tuple-element.18, f32[2,2,16]{2,1,0:T(2,128)S(1)} %multiply_maximum_fusion, f32[2,2,16]{2,1,0:T(2,128)S(1)} %get-tuple-element.7, f32[2,2,128]{2,1,0:T(2,128)S(1)} %slice_bitcast_fusion, ...), kind=kOutput, calls=%fused_computation.10 | convolution fusion | flops 16941056 | bytes 1329920 | tf_op jit(solution)/shard_map/mrkgs,mrskd->mrkgd/dot_general | solution.py:53
  59.4 13.1 %all_gather.3 = bf16[2,8,2048]{2,0,1:T(2,128)(2,1)S(1)} all-gather(bf16[2,2,2048]{2,0,1:T(2,128)(2,1)S(1)} %copy.12), channel_id=1, replica_groups=mesh['groups'=2,'gx'=4,'gy'=4] {'gx'}, dimensions={1}, use_global_device_ids=true | all-gather | bytes 81920 | tf_op jit(solution)/shard_map/all_gather | solution.py:83
  72.6 8.8 %fusion = f32[2,8,4096]{2,1,0:T(8,128)} fusion(bf16[2048,4096]{1,0:T(8,128)(2,1)} %param.12, bf16[2,8,2048]{2,0,1:T(2,128)(2,1)S(1)} %all_gather.3), kind=kOutput, calls=%fused_computation | convolution fusion | flops 268435456 | bytes 17104896 | tf_op jit(solution)/shard_map/mrc,cd->mrd/dot_general | solution.py:81
  81.3 0.0 all-reduce.7.cloned.1.call-update
  81.3 32.2 %all-reduce.7.cloned.1.call-done = f32[2,8,4096]{2,1,0:T(8,128)} async-done(((f32[2,8,4096]{2,1,0:T(8,128)}), f32[2,8,4096]{2,1,0:T(8,128)}) %all-reduce.7.cloned.1.call-update) | async-done | bytes 262160 | tf_op jit(solution)/shard_map/psum | solution.py:87
  113.5 1.6 %fusion.14 = bf16[2,8,4096]{2,1,0:T(8,128)(2,1)} fusion(f32[2,8,4096]{2,1,0:T(8,128)} %all-reduce.7.cloned.1.call-done, bf16[2,8,4096]{2,1,0:T(8,128)(2,1)S(1)} %copy-done.1), kind=kLoop, calls=%fused_computation.19 | loop fusion | flops 196608 | bytes 524288 | tf_op jit(solution)/shard_map/convert_element_type | solution.py:88
  (8 shorter events, 0.1 us)
Async XLA Ops:
  6.5 10.0 %copy-start = (bf16[4096,1,256]{2,0,1:T(8,128)(2,1)S(1)}, bf16[4096,1,256]{2,0,1:T(8,128)(2,1)}, u32[]{:S(2)}) copy-start(bf16[4096,1,256]{2,0,1:T(8,128)(2,1)} %param.11) | copy-start | bytes 6291460
  6.5 47.3 %all-reduce.9.cloned.1.call-start = ((), (), s32[]{:S(2)}) async-start(), calls=%async_computation.1 | async-start | bytes 262144
  7.4 8.9 %copy-start.1 = (bf16[2,8,4096]{2,1,0:T(8,128)(2,1)S(1)}, bf16[2,8,4096]{2,1,0:T(8,128)(2,1)}, u32[]{:S(2)}) copy-start(bf16[2,8,4096]{2,1,0:T(8,128)(2,1)} %param.7) | copy-start | bytes 393220
  7.4 9.0 %copy-start.2 = (s32[2,2]{1,0:T(2,128)S(1)}, s32[2,2]{1,0:T(2,128)}, u32[]{:S(2)}) copy-start(s32[2,2]{1,0:T(2,128)} %param.8) | copy-start | bytes 52
  16.2 0.7 copy-start.3
  16.2 97.3 %all-reduce.7.cloned.1.call-start = ((), (), s32[]{:S(2)}) async-start(), calls=%async_computation | async-start | bytes 524288 | tf_op jit(solution)/shard_map/psum | solution.py:87
Sparse Core Ops, SparseCore 0:
  16.4 37.4 all-reduce.8
  81.5 31.9 all-reduce.6
where the time goes:
time: 122 us
  waiting for transfers between devices  39.5 us (32%)
  blocking collectives  33.9 us (28%)
  matrix products  22 us (18%)
  between operations  14.2 us (12%)
  local copies, waits for them, and re-layouts  8.61 us (7%)
  other arithmetic  3.71 us (3%)
    psum x1, waiting for transfers between devices, local(): summed_heads = lax.psum(projected, 'gy')  32.2 us
    unnamed x1, blocking collectives  20.8 us
    all_gather x1, blocking collectives, local(): lax.all_gather(attended, 'gx', axis=1, tiled=True)  13.1 us
    dot_general x1, matrix products, local(): jnp.einsum('mrd,dc->mrc', normed, w_query, preferred_element_type=jnp.flo...  8.81 us
    dot_general x1, matrix products, local(): jnp.einsum('mrc,cd->mrd', lax.all_gather(attended, 'gx', axis=1, tiled=Tr...  8.75 us
    unnamed x3, waiting for transfers between devices  7.38 us
    slice x1, local copies, waits for them, and re-layouts, attend(): keys = cache[:, :, :, :, 0, :]  6.95 us
  transfers between devices with their start and end apart: 2, of which 2 were waited for; matrix products, arithmetic and copies ran while one was open for 7% of the time, Pallas kernels for 0%

commit v1 on v0

--- a/solution.py
+++ b/solution.py
@@ -80,7 +80,7 @@
     attended = attend(query_sum, keyval_sum, local_squares, lengths, cache)
     projected = jnp.einsum(
         "mrc,cd->mrd",
-        lax.all_gather(attended, "gx", axis=1, tiled=True),
+        jnp.concatenate(lax.all_gather(attended, "gx"), axis=1),
         w_out,
         preferred_element_type=jnp.float32,
     )

time: 122 us -> 122 us (level)
  no operation moved by 1% of the time
where the time goes in v1:
time: 122 us
  waiting for transfers between devices  39.5 us (32%)
  blocking collectives  33.9 us (28%)
  matrix products  21.9 us (18%)
  between operations  14.2 us (12%)
  local copies, waits for them, and re-layouts  8.68 us (7%)
  other arithmetic  3.71 us (3%)
    psum x1, waiting for transfers between devices, local(): summed_heads = lax.psum(projected, 'gy')  32.2 us
    unnamed x1, blocking collectives  20.8 us
    all_gather x1, blocking collectives, local(): lax.all_gather(attended, 'gx')  13.1 us
    dot_general x1, matrix products, local(): jnp.einsum('mrd,dc->mrc', normed, w_query, preferred_element_type=jnp.flo...  8.81 us
    dot_general x1, matrix products, local(): jnp.einsum('mrc,cd->mrd', jnp.concatenate(lax.all_gather(attended, 'gx'),...  8.75 us
    unnamed x3, waiting for transfers between devices  7.38 us
    slice x1, local copies, waits for them, and re-layouts, attend(): keys = cache[:, :, :, :, 0, :]  6.95 us
  transfers between devices with their start and end apart: 2, of which 2 were waited for; matrix products, arithmetic and copies ran while one was open for 7% of the time, Pallas kernels for 0%

profile of v1, /device:TPU:0, one launch (start us, length us, event | category | flops | bytes accessed | tf_op | source)
XLA Modules:
  0.0 122.0 jit_solution(14115741514442153627)
XLA Ops:
  6.5 0.0 copy-start
  6.5 0.0 all-reduce.9.cloned.1.call-start
  6.5 0.8 convert_element_type.46
  7.4 0.0 copy-start.1
  7.4 0.0 copy-start.2
  7.4 8.8 %fusion.2 = f32[2,8,2048]{2,1,0:T(8,128)} fusion(bf16[4096,2048]{1,0:T(8,128)(2,1)} %param.10, bf16[2,8,4096]{2,1,0:T(8,128)(2,1)} %param.7, f32[4096]{0:T(1024)S(1)} %convert_element_type.46), kind=kOutput, calls=%fused_computation.2 | convolution fusion | flops 268632064 | bytes 17055744 | tf_op jit(solution)/shard_map/mrd,dc->mrc/dot_general | solution.py:71
  16.2 0.0 copy-start.3
  16.2 0.0 all-reduce.9.cloned.1.call-update
  16.2 0.0 all-reduce.7.cloned.1.call-start
  16.3 0.0 copy-done.1
  16.3 0.1 fusion.13
  16.4 0.0 copy-done.2
  16.4 0.1 iota_compare_fusion
  16.5 0.0 copy-done
  16.5 0.4 fusion.9
  16.9 0.0 copy-done.3
  16.9 0.7 dynamic-slice
  18.3 0.1 multiply_cosine_fusion.1
  18.4 20.8 %all-reduce.3 = (f32[2,8]{1,0:T(2,128)S(1)}, f32[2,8,1,256]{3,1,0,2:T(8,128)S(1)}) all-reduce(f32[2,8]{1,0:T(2,128)S(1)} %fusion.13, f32[2,8,1,256]{3,1,0,2:T(8,128)S(1)} %fusion.9), channel_id=3, replica_groups=mesh['groups'=2,'gx'=4,'gy'=4] {'gx'}, use_global_device_ids=true, to_apply=%region_2.0.clone | all-reduce | flops 4112 | bytes 32896
  39.2 0.1 fusion.31
  39.3 0.1 dynamic-slice_multiply_fusion
  39.4 0.1 fusion.28
  39.5 6.9 %fusion.34 = (bf16[2,2,1024,1,1,128]{5,4,3,2,1,0:T(2,128)(2,1)}, bf16[2,2,1024,1,1,128]{5,4,3,2,1,0:T(2,128)(2,1)}) fusion(bf16[2,2,1024,1,2,128]{5,4,3,2,1,0:T(2,128)(2,1)} %param.13), kind=kLoop, calls=%fused_computation.54 | loop fusion | bytes 4194304 | tf_op jit(solution)/shard_map/slice | solution.py:38
  46.4 0.1 maximum_bitcast_fusion
  46.5 7.3 %all-reduce.9.cloned.1.call-done = f32[2,8,2048]{2,1,0:T(8,128)} async-done(((f32[2,8,2048]{2,1,0:T(8,128)}), f32[2,8,2048]{2,1,0:T(8,128)}) %all-reduce.9.cloned.1.call-update) | async-done | bytes 131088
  53.9 0.9 constant_dynamic-slice_fusion
  54.8 0.1 broadcast_multiply_fusion
  54.9 0.1 subtract_convert_fusion
  55.0 0.2 multiply_reduce_fusion
  55.1 2.1 %fusion.35 = (f32[2,2,16]{2,1,0:T(2,128)S(1)}, f32[2,2,16,1024]{3,2,1,0:T(8,128)S(1)}) fusion(bf16[2,2,1024,1,1,128]{5,4,3,2,1,0:T(2,128)(2,1)} %get-tuple-element.9, bf16[2,2,16,64]{3,2,1,0:T(8,128)(2,1)S(1)} %bitcast.41, bf16[2,2,16,64]{3,2,1,0:T(8,128)(2,1)S(1)} %bitcast.40, pred[2,2,1024]{2,1,0:T(4,128)(4,1)S(1)} %iota_compare_fusion), kind=kOutput, calls=%fused_computation.55 | convolution fusion | flops 17006528 | bytes 1331456 | tf_op jit(solution)/shard_map/mrkgd,mrskd->mrkgs/dot_general | solution.py:41
  57.3 0.2 fusion.15
  57.5 1.9 %fusion.8 = bf16[2,2,16,128]{3,2,1,0:T(8,128)(2,1)S(1)} fusion(bf16[2,2,1024,1,1,128]{5,4,3,2,1,0:T(2,128)(2,1)} %get-tuple-element.10, f32[2,2,16,1024]{3,2,1,0:T(8,128)S(1)} %get-tuple-element.18, f32[2,2,16]{2,1,0:T(2,128)S(1)} %multiply_maximum_fusion, f32[2,2,16]{2,1,0:T(2,128)S(1)} %get-tuple-element.7, f32[2,2,128]{2,1,0:T(2,128)S(1)} %slice_bitcast_fusion, ...), kind=kOutput, calls=%fused_computation.10 | convolution fusion | flops 16941056 | bytes 1329920 | tf_op jit(solution)/shard_map/mrkgs,mrskd->mrkgd/dot_general | solution.py:53
  59.4 13.1 %all_gather.3 = bf16[4,2,2,2048]{3,2,1,0:T(2,128)(2,1)S(1)} all-gather(bf16[1,2,2,2048]{3,2,1,0:T(2,128)(2,1)S(1)} %all_gather_reshape.3), channel_id=1, replica_groups=mesh['groups'=2,'gx'=4,'gy'=4] {'gx'}, dimensions={0}, use_global_device_ids=true | all-gather | bytes 81920 | tf_op jit(solution)/shard_map/all_gather | solution.py:83
  72.6 8.7 %fusion = f32[2,8,4096]{2,1,0:T(8,128)} fusion(bf16[2,8,2048]{2,1,0:T(8,128)(2,1)S(1)} %reshape.203, bf16[2048,4096]{1,0:T(8,128)(2,1)} %param.12), kind=kOutput, calls=%fused_computation | convolution fusion | flops 268435456 | bytes 17104896 | tf_op jit(solution)/shard_map/mrc,cd->mrd/dot_general | solution.py:81
  81.4 0.0 all-reduce.7.cloned.1.call-update
  81.4 32.2 %all-reduce.7.cloned.1.call-done = f32[2,8,4096]{2,1,0:T(8,128)} async-done(((f32[2,8,4096]{2,1,0:T(8,128)}), f32[2,8,4096]{2,1,0:T(8,128)}) %all-reduce.7.cloned.1.call-update) | async-done | bytes 262160 | tf_op jit(solution)/shard_map/psum | solution.py:87
  113.6 1.6 %fusion.14 = bf16[2,8,4096]{2,1,0:T(8,128)(2,1)} fusion(f32[2,8,4096]{2,1,0:T(8,128)} %all-reduce.7.cloned.1.call-done, bf16[2,8,4096]{2,1,0:T(8,128)(2,1)S(1)} %copy-done.1), kind=kLoop, calls=%fused_computation.19 | loop fusion | flops 196608 | bytes 524288 | tf_op jit(solution)/shard_map/convert_element_type | solution.py:88
  (9 shorter events, 0.2 us)
Async XLA Ops:
  6.5 10.0 %copy-start = (bf16[4096,1,256]{2,0,1:T(8,128)(2,1)S(1)}, bf16[4096,1,256]{2,0,1:T(8,128)(2,1)}, u32[]{:S(2)}) copy-start(bf16[4096,1,256]{2,0,1:T(8,128)(2,1)} %param.11) | copy-start | bytes 6291460
  6.5 47.3 %all-reduce.9.cloned.1.call-start = ((), (), s32[]{:S(2)}) async-start(), calls=%async_computation.1 | async-start | bytes 262144
  7.4 8.9 %copy-start.1 = (bf16[2,8,4096]{2,1,0:T(8,128)(2,1)S(1)}, bf16[2,8,4096]{2,1,0:T(8,128)(2,1)}, u32[]{:S(2)}) copy-start(bf16[2,8,4096]{2,1,0:T(8,128)(2,1)} %param.7) | copy-start | bytes 393220
  7.4 9.0 %copy-start.2 = (s32[2,2]{1,0:T(2,128)S(1)}, s32[2,2]{1,0:T(2,128)}, u32[]{:S(2)}) copy-start(s32[2,2]{1,0:T(2,128)} %param.8) | copy-start | bytes 52
  16.2 0.7 copy-start.3
  16.2 97.3 %all-reduce.7.cloned.1.call-start = ((), (), s32[]{:S(2)}) async-start(), calls=%async_computation | async-start | bytes 524288 | tf_op jit(solution)/shard_map/psum | solution.py:87
Sparse Core Ops, SparseCore 0:
  16.4 37.4 all-reduce.8
  81.5 31.9 all-reduce.6
